TPU v7x, 32 devices: a whole 2x2x4 slice. The times are simulated.
32 devices in a mesh: fsdp: 8 (over z, x), dp: 4 (over y, core).
Axes of the slice: x: 2, y: 2, z: 4, core: 2. Of those that a mesh axis runs over, the one named last changes fastest.
Arguments:
- features: bfloat16 [8192, 1024], P(('fsdp', 'dp')), may hold values from -6 to 6
- normed: bfloat16 [8192, 4096], P(('fsdp', 'dp')), may hold values from -6 to 6
- relu_mask: int32 [8192, 4096], P(('fsdp', 'dp')), may hold values 0 or 1
- cotangent: bfloat16 [8192, 4096], P(('fsdp', 'dp')), may hold values from -40 to 40
- weight_shard: bfloat16 [1024, 4096], P('fsdp'), may hold values from -0.1875 to 0.1875
- norm_gain: float32 [4096], replicated, may hold values from 0.25 to 1.75
- inverse_deviation: float32 [4096], replicated, may hold values from 0.5 to 3
Outputs:
- grad_input: bfloat16 [8192, 1024], P(('fsdp', 'dp'))
- grad_weight: float32 [1024, 4096], P('fsdp')
- grad_gain: float32 [4096], replicated
- grad_shift: float32 [4096], replicated
All inputs are finite; a program needn't handle non-finite values. No bound on the sum of `relu_mask` on one device may be relied on, other than what follows from the above.
Results may differ from a plain program's by a relative error of at most 0.005.
Values may be sent and summed in bfloat16 or wider, within the bound.
No kernel may reach another device: no remote copies, remote signals or barrier semaphores. Data moves between devices by JAX's collectives and lax.ppermute only.
A program may use at most 128 MiB of HBM per device.

v0:
```python
import math
import jax
import jax.numpy as jnp
from jax import lax
from jax.sharding import PartitionSpec as P


def on_device(features, normed, relu_mask, cotangent, weight_shard, norm_gain, inverse_deviation):
    local_rows = features.shape[0]
    total_rows = local_rows * lax.axis_size("fsdp") * lax.axis_size("dp")
    masked = cotangent.astype(jnp.float32) * relu_mask.astype(jnp.float32)
    normed_f = normed.astype(jnp.float32)
    local_plain = jnp.sum(masked, axis=0)
    local_cross = jnp.sum(masked * normed_f, axis=0)
    sum_plain, sum_cross = lax.psum((local_plain, local_cross), ("fsdp", "dp"))
    norm_grad = (
        inverse_deviation
        * norm_gain
        * (masked - sum_plain / total_rows - normed_f * (sum_cross / total_rows))
    )
    norm_grad = norm_grad.astype(jnp.bfloat16)
    grad_input = lax.dot_general(
        norm_grad,
        lax.all_gather(weight_shard, "fsdp", axis=0, tiled=True),
        (((1,), (1,)), ((), ())),
        preferred_element_type=jnp.float32,
    ).astype(jnp.bfloat16)
    unit_block = lax.all_to_all(norm_grad, "dp", split_axis=1, concat_axis=0, tiled=True)
    unit_term = lax.dot_general(
        lax.all_gather(features, "dp", axis=0, tiled=True),
        unit_block,
        (((0,), (0,)), ((), ())),
        preferred_element_type=jnp.float32,
    )
    owner_part = lax.psum_scatter(unit_term, "fsdp", scatter_dimension=0, tiled=True)
    summed = lax.all_gather(owner_part, "dp", axis=1, tiled=True)
    rescale = 1.0 / math.sqrt(total_rows)
    return (grad_input, summed * rescale, sum_cross * rescale, sum_plain * rescale)


def solution(mesh):
    in_specs = (
        P(("fsdp", "dp"), None),
        P(("fsdp", "dp"), None),
        P(("fsdp", "dp"), None),
        P(("fsdp", "dp"), None),
        P("fsdp", None),
        P(),
        P(),
    )
    out_specs = (P(("fsdp", "dp"), None), P("fsdp", None), P(), P())
    return jax.shard_map(
        on_device, mesh=mesh, in_specs=in_specs, out_specs=out_specs, check_vma=False
    )
```

profile of v0, /device:TPU:0, one launch (start us, length us, event | category | flops | bytes accessed | tf_op | source)
XLA Modules:
  0.0 361.4 jit_solution(14963796621022647305)
XLA Ops:
  7.2 0.0 all-gather.6.cloned.1.call-start
  7.2 0.7 all-gather.6.cloned.1.call-update
  7.9 0.0 reduce-scatter.2.cloned.1.call-start
  7.9 3.3 copy.15
  11.2 5.6 %copy.14 = s32[256,4096]{0,1:T(8,128)} copy(s32[256,4096]{1,0:T(8,128)} %param.9) | data formatting | bytes 8388608 | tf_op args[2]
  16.8 4.1 %copy.13 = bf16[256,4096]{0,1:T(8,128)(2,1)} copy(bf16[256,4096]{1,0:T(8,128)(2,1)} %param.10) | data formatting | bytes 4194304 | tf_op args[3]
  21.0 0.0 copy-start.2
  21.0 0.0 copy-start.3
  21.0 4.1 %fusion.4 = (f32[4096]{0:T(1024)S(1)}, f32[4096]{0:T(1024)S(1)}) fusion(s32[256,4096]{0,1:T(8,128)} %copy.14, bf16[256,4096]{0,1:T(8,128)(2,1)} %copy.13, bf16[256,4096]{0,1:T(8,128)(2,1)S(1)} %copy.15), kind=kLoop, calls=%fused_computation.8 | loop fusion | flops 7331840 | bytes 8421376 | tf_op jit(solution)/shard_map/reduce_sum | solution.py:13
  25.1 0.0 copy-done.2
  25.1 0.0 copy-done.3
  25.1 42.3 %all-reduce = (f32[4096]{0:T(1024)S(1)}, f32[4096]{0:T(1024)S(1)}) all-reduce(f32[4096]{0:T(1024)S(1)} %get-tuple-element.17, f32[4096]{0:T(1024)S(1)} %get-tuple-element.16), channel_id=1, replica_groups=mesh['fsdp'=8,'dp'=4] {'fsdp','dp'}, use_global_device_ids=true, to_apply=%region_3.0 | all-reduce | flops 8192 | bytes 65536 | tf_op jit(solution)/shard_map/psum | solution.py:15
  67.4 0.6 broadcast_multiply_fusion.1
  68.0 4.3 %fusion.3 = bf16[256,4096]{0,1:T(8,128)(2,1)S(1)} fusion(bf16[256,4096]{0,1:T(8,128)(2,1)S(1)} %copy.15, f32[4096]{0:T(1024)S(1)} %get-tuple-element.24, f32[4096]{0:T(1024)S(1)} %get-tuple-element.21, f32[4096]{0:T(1024)S(1)} %mul.37, s32[256,4096]{0,1:T(8,128)} %copy.14, bf16[256,4096]{0,1:T(8,128)(2,1)} %copy.13), kind=kLoop, calls=%fused_computation.5 | loop fusion | flops 9437184 | bytes 10534912 | tf_op jit(solution)/shard_map/convert_element_type | solution.py:21
  72.3 0.0 copy-start
  72.3 29.0 %all_to_all.19 = bf16[256,4,1024]{0,2,1:T(8,128)(2,1)S(1)} all-to-all(bf16[256,4,1024]{0,2,1:T(8,128)(2,1)S(1)} %bitcast.9), channel_id=1, replica_groups=mesh['fsdp'=8,'dp'=4] {'dp'}, dimensions={1} | all-to-all | bytes 4194304 | tf_op jit(solution)/shard_map/all_to_all | solution.py:28
  101.3 0.0 copy-done
  101.3 2.4 copy.16
  103.7 0.0 all-gather.6.cloned.1.call-done
  103.7 6.5 %convolution_bitcast_fusion = f32[1024,1024]{0,1:T(8,128)} fusion(bf16[1024,1024]{1,0:T(8,128)(2,1)} %bitcast.11, bf16[1024,1024]{1,0:T(8,128)(2,1)} %all-gather.6.cloned.1.call-done), kind=kOutput, calls=%fused_computation.7 | convolution fusion | flops 2147483648 | bytes 8388608 | tf_op jit(solution)/shard_map/dot_general | solution.py:29
  110.3 0.0 reduce-scatter.2.cloned.1.call-update
  110.3 0.0 all-gather.8.cloned.1.call-start
  110.3 87.7 %reduce-scatter.2.cloned.1.call-done = f32[128,1024]{0,1:T(8,128)} async-done(((f32[1024,1024]{0,1:T(8,128)}), f32[128,1024]{0,1:T(8,128)}) %reduce-scatter.2.cloned.1.call-update) | async-done | bytes 524304 | tf_op jit(solution)/shard_map/reduce_scatter | solution.py:35
  198.0 0.0 all-gather.8.cloned.1.call-update
  198.1 0.0 all-gather.4.cloned.1.call-start
  198.1 0.5 all-gather.4.cloned.1.call-update
  198.6 23.2 %all-gather.8.cloned.1.call-done = f32[128,4096]{0,1:T(8,128)} async-done(((f32[128,1024]{0,1:T(8,128)}), f32[128,4096]{0,1:T(8,128)}) %all-gather.8.cloned.1.call-update) | async-done | bytes 2097168 | tf_op jit(solution)/shard_map/all_gather | solution.py:36
  221.8 3.1 broadcast_multiply_fusion
  224.9 3.0 copy.17
  227.9 120.4 %all-gather.4.cloned.1.call-done = bf16[1024,4096]{1,0:T(8,128)(2,1)} async-done(((bf16[128,4096]{1,0:T(8,128)(2,1)}), bf16[1024,4096]{1,0:T(8,128)(2,1)}) %all-gather.4.cloned.1.call-update) | async-done | bytes 8388624 | tf_op jit(solution)/shard_map/all_gather | solution.py:24
  348.3 0.0 copy-done.1
  348.3 6.6 %convolution_convert_fusion = bf16[256,1024]{1,0:T(8,128)(2,1)} fusion(bf16[256,4096]{0,1:T(8,128)(2,1)S(1)} %copy-done.1, bf16[1024,4096]{1,0:T(8,128)(2,1)} %all-gather.4.cloned.1.call-done), kind=kOutput, calls=%fused_computation.9 | convolution fusion | flops 2147745792 | bytes 11010048 | tf_op jit(solution)/shard_map/dot_general | solution.py:22
  (2 shorter events, 0.0 us)
Async XLA Ops:
  7.2 96.6 %all-gather.6.cloned.1.call-start = ((), (), s32[]{:S(2)}) async-start(), calls=%async_computation.3 | async-start | bytes 2621440 | tf_op jit(solution)/shard_map/all_gather | solution.py:30
  7.9 190.1 %reduce-scatter.2.cloned.1.call-start = ((), (), s32[]{:S(2)}) async-start(), calls=%async_computation.4 | async-start | bytes 4718592 | tf_op jit(solution)/shard_map/reduce_scatter | solution.py:35
  21.0 4.1 %copy-start.2 = (f32[4096]{0:T(1024)S(1)}, f32[4096]{0:T(1024)}, u32[]{:S(2)}) copy-start(f32[4096]{0:T(1024)} %param.13) | copy-start | bytes 49156
  21.0 4.1 %copy-start.3 = (f32[4096]{0:T(1024)S(1)}, f32[4096]{0:T(1024)}, u32[]{:S(2)}) copy-start(f32[4096]{0:T(1024)} %param.12) | copy-start | bytes 49156
  72.3 29.0 %copy-start = (bf16[256,4096]{0,1:T(8,128)(2,1)}, bf16[256,4096]{0,1:T(8,128)(2,1)S(1)}, u32[]{:S(2)}) copy-start(bf16[256,4096]{0,1:T(8,128)(2,1)S(1)} %fusion.3) | copy-start | bytes 6291460
  110.3 111.5 %all-gather.8.cloned.1.call-start = ((), (), s32[]{:S(2)}) async-start(), calls=%async_computation.5 | async-start | bytes 2621440 | tf_op jit(solution)/shard_map/all_gather | solution.py:36
  198.1 150.2 %all-gather.4.cloned.1.call-start = ((), (), s32[]{:S(2)}) async-start(), calls=%async_computation.2 | async-start | bytes 9437184 | tf_op jit(solution)/shard_map/all_gather | solution.py:24
  224.9 123.4 %copy-start.1 = (bf16[256,4096]{0,1:T(8,128)(2,1)S(1)}, bf16[256,4096]{0,1:T(8,128)(2,1)}, u32[]{:S(2)}) copy-start(bf16[256,4096]{0,1:T(8,128)(2,1)} %copy-done) | copy-start | bytes 6291460
Sparse Core Ops, SparseCore 0:
  9.5 25.2 all-gather.5
  110.4 87.5 reduce-scatter.1
  199.6 22.1 all-gather.7
  223.8 124.4 all-gather.3
where the time goes:
time: 362 us; the launch traced here: 361 us
  waiting for transfers between devices  232 us (64%)
  blocking collectives  71.3 us (20%)
  local copies, waits for them, and re-layouts  18.4 us (5%)
  between operations  13.8 us (4%)
  matrix products  13.1 us (4%)
  other arithmetic  12.1 us (3%)
    all_gather x1, waiting for transfers between devices, on_device(): lax.all_gather(weight_shard, 'fsdp', axis=0, tiled=True)  120 us
    reduce_scatter x1, waiting for transfers between devices, on_device(): lax.psum_scatter(unit_term, 'fsdp', scatter_dimension=0, tiled=True)  87.7 us
    psum x1, blocking collectives, on_device(): sum_plain, sum_cross = lax.psum((local_plain, local_cross), ('fsdp', 'dp'))  42.3 us
    all_to_all x1, blocking collectives, on_device(): lax.all_to_all(norm_grad, 'dp', split_axis=1, concat_axis=0, tiled=True)  29 us
    all_gather x1, waiting for transfers between devices, on_device(): summed = lax.all_gather(owner_part, 'dp', axis=1, tiled=True)  23.2 us
    unnamed x12, local copies, waits for them, and re-layouts  16.1 us
  transfers between devices with their start and end apart: 4, of which 3 were waited for; matrix products, arithmetic and copies ran while one was open for 8% of the time, Pallas kernels for 0%

commit v1 on v0

--- a/solution.py
+++ b/solution.py
@@ -3,6 +3,16 @@
 import jax.numpy as jnp
 from jax import lax
 from jax.sharding import PartitionSpec as P
+
+
+def around_the_ring(x, mesh_axis, dim):
+    devices = lax.axis_size(mesh_axis)
+    held, shards = (x, [x])
+    for _ in range(devices - 1):
+        held = lax.ppermute(held, mesh_axis, [(i, (i + 1) % devices) for i in range(devices)])
+        shards.insert(0, held)
+    line = jnp.concatenate(shards, axis=dim)
+    return jnp.roll(line, (lax.axis_index(mesh_axis) + 1) * x.shape[dim], axis=dim)
 
 
 def on_device(features, normed, relu_mask, cotangent, weight_shard, norm_gain, inverse_deviation):
@@ -33,7 +43,7 @@
         preferred_element_type=jnp.float32,
     )
     owner_part = lax.psum_scatter(unit_term, "fsdp", scatter_dimension=0, tiled=True)
-    summed = lax.all_gather(owner_part, "dp", axis=1, tiled=True)
+    summed = around_the_ring(owner_part, "dp", 1)
     rescale = 1.0 / math.sqrt(total_rows)
     return (grad_input, summed * rescale, sum_cross * rescale, sum_plain * rescale)
 

time: 362 us -> 339 us (0.936)
  waiting for transfers between devices: 232 us -> 209 us
    ppermute x0 -> x3, waiting for transfers between devices: none -> 26 us  [around_the_ring(): lax.ppermute(held, mesh_axis, [(i, (i + 1) % devices) for i in range(devi...]
    all_gather x1, waiting for transfers between devices: 120 us -> 94.4 us  [on_device(): lax.all_gather(weight_shard, 'fsdp', axis=0, tiled=True)]
    all_gather x1 -> x0, waiting for transfers between devices: 23.2 us -> none  [on_device(): summed = lax.all_gather(owner_part, 'dp', axis=1, tiled=True)]
    unnamed x12 -> x21, local copies, waits for them, and re-layouts: 16.1 us -> 18.5 us
  transfers between devices with their start and end apart: 4 -> 6, of which waited for: 3 -> 5; matrix products, arithmetic and copies ran while one was open for 8% -> 9% of each run, Pallas kernels for 0% -> 0%
where the time goes in v1:
time: 339 us
  waiting for transfers between devices  209 us (62%)
  blocking collectives  71.2 us (21%)
  local copies, waits for them, and re-layouts  20.9 us (6%)
  between operations  13.9 us (4%)
  matrix products  13.1 us (4%)
  other arithmetic  10.5 us (3%)
    all_gather x1, waiting for transfers between devices, on_device(): lax.all_gather(weight_shard, 'fsdp', axis=0, tiled=True)  94.4 us
    reduce_scatter x1, waiting for transfers between devices, on_device(): lax.psum_scatter(unit_term, 'fsdp', scatter_dimension=0, tiled=True)  87.1 us
    psum x1, blocking collectives, on_device(): sum_plain, sum_cross = lax.psum((local_plain, local_cross), ('fsdp', 'dp'))  42.2 us
    all_to_all x1, blocking collectives, on_device(): lax.all_to_all(norm_grad, 'dp', split_axis=1, concat_axis=0, tiled=True)  29 us
    ppermute x3, waiting for transfers between devices, around_the_ring(): lax.ppermute(held, mesh_axis, [(i, (i + 1) % devices) for i in range(devi...  26 us
    unnamed x21, local copies, waits for them, and re-layouts  18.5 us
  transfers between devices with their start and end apart: 6, of which 5 were waited for; matrix products, arithmetic and copies ran while one was open for 9% of the time, Pallas kernels for 0%

profile of v1, /device:TPU:0, one launch (start us, length us, event | category | flops | bytes accessed | tf_op | source)
XLA Modules:
  0.0 338.7 jit_solution(16744825231512493808)
XLA Ops:
  7.2 0.0 all-gather.5.cloned.1.call-start
  7.2 0.7 all-gather.5.cloned.1.call-update
  7.9 0.0 reduce-scatter.2.cloned.1.call-start
  7.9 3.3 copy.15
  11.2 5.6 %copy.14 = s32[256,4096]{0,1:T(8,128)} copy(s32[256,4096]{1,0:T(8,128)} %param.9) | data formatting | bytes 8388608 | tf_op args[2]
  16.8 4.1 %copy.13 = bf16[256,4096]{0,1:T(8,128)(2,1)} copy(bf16[256,4096]{1,0:T(8,128)(2,1)} %param.10) | data formatting | bytes 4194304 | tf_op args[3]
  21.0 4.1 %fusion.4 = (f32[4096]{0:T(1024)S(1)}, f32[4096]{0:T(1024)S(1)}) fusion(s32[256,4096]{0,1:T(8,128)} %copy.14, bf16[256,4096]{0,1:T(8,128)(2,1)} %copy.13, bf16[256,4096]{0,1:T(8,128)(2,1)S(1)} %copy.15), kind=kLoop, calls=%fused_computation.9 | loop fusion | flops 7331840 | bytes 8421376 | tf_op jit(solution)/shard_map/reduce_sum | solution.py:23
  25.0 0.0 copy-done.4
  25.1 42.2 %all-reduce = (f32[4096]{0:T(1024)S(1)}, f32[4096]{0:T(1024)S(1)}) all-reduce(f32[4096]{0:T(1024)S(1)} %get-tuple-element.17, f32[4096]{0:T(1024)S(1)} %get-tuple-element.16), channel_id=1, replica_groups=mesh['fsdp'=8,'dp'=4] {'fsdp','dp'}, use_global_device_ids=true, to_apply=%region_3.0 | all-reduce | flops 8192 | bytes 65536 | tf_op jit(solution)/shard_map/psum | solution.py:25
  67.3 0.6 broadcast_multiply_fusion
  67.9 4.3 %fusion.3 = bf16[256,4096]{0,1:T(8,128)(2,1)S(1)} fusion(bf16[256,4096]{0,1:T(8,128)(2,1)S(1)} %copy.15, f32[4096]{0:T(1024)S(1)} %get-tuple-element.24, f32[4096]{0:T(1024)S(1)} %get-tuple-element.21, f32[4096]{0:T(1024)S(1)} %mul.40, s32[256,4096]{0,1:T(8,128)} %copy.14, bf16[256,4096]{0,1:T(8,128)(2,1)} %copy.13), kind=kLoop, calls=%fused_computation.5 | loop fusion | flops 9437184 | bytes 10534912 | tf_op jit(solution)/shard_map/convert_element_type | solution.py:31
  72.2 0.0 copy-start
  72.2 1.3 copy-done
  73.5 29.0 %all_to_all.19 = bf16[256,4,1024]{0,2,1:T(8,128)(2,1)S(1)} all-to-all(bf16[256,4,1024]{0,2,1:T(8,128)(2,1)S(1)} %bitcast.9), channel_id=1, replica_groups=mesh['fsdp'=8,'dp'=4] {'dp'}, dimensions={1} | all-to-all | bytes 4194304 | tf_op jit(solution)/shard_map/all_to_all | solution.py:38
  102.6 2.4 copy.16
  104.9 6.6 %convolution_bitcast_fusion = f32[1024,1024]{0,1:T(8,128)} fusion(bf16[1024,1024]{1,0:T(8,128)(2,1)} %bitcast.11, bf16[1024,1024]{1,0:T(8,128)(2,1)} %all-gather.5.cloned.1.call-done), kind=kOutput, calls=%fused_computation.7 | convolution fusion | flops 2147483648 | bytes 8388608 | tf_op jit(solution)/shard_map/dot_general | solution.py:39
  111.5 0.0 reduce-scatter.2.cloned.1.call-update
  111.5 0.0 all-gather.3.cloned.1.call-start
  111.6 0.7 all-gather.3.cloned.1.call-update
  112.2 87.1 %reduce-scatter.2.cloned.1.call-done = f32[128,1024]{0,1:T(8,128)} async-done(((f32[1024,1024]{0,1:T(8,128)}), f32[128,1024]{0,1:T(8,128)}) %reduce-scatter.2.cloned.1.call-update) | async-done | bytes 524304 | tf_op jit(solution)/shard_map/reduce_scatter | solution.py:45
  199.4 0.0 collective-permute-start
  199.4 8.8 %collective-permute-done = f32[128,1024]{0,1:T(8,128)S(1)} collective-permute-done((f32[128,1024]{0,1:T(8,128)}, f32[128,1024]{0,1:T(8,128)S(1)}, u32[]{:S(2)}, u32[]{:S(2)}) %collective-permute-start) | collective-permute-done | bytes 524320 | tf_op jit(solution)/shard_map/ppermute | solution.py:12
  208.2 0.0 collective-permute-start.1
  208.2 8.6 %collective-permute-done.1 = f32[128,1024]{0,1:T(8,128)S(1)} collective-permute-done((f32[128,1024]{0,1:T(8,128)S(1)}, f32[128,1024]{0,1:T(8,128)S(1)}, u32[]{:S(2)}, u32[]{:S(2)}) %collective-permute-start.1) | collective-permute-done | bytes 524320 | tf_op jit(solution)/shard_map/ppermute | solution.py:12
  216.8 0.0 collective-permute-start.2
  216.8 8.6 %collective-permute-done.2 = f32[128,1024]{0,1:T(8,128)S(1)} collective-permute-done((f32[128,1024]{0,1:T(8,128)S(1)}, f32[128,1024]{0,1:T(8,128)S(1)}, u32[]{:S(2)}, u32[]{:S(2)}) %collective-permute-start.2) | collective-permute-done | bytes 524320 | tf_op jit(solution)/shard_map/ppermute | solution.py:12
  225.5 1.1 constant_dynamic-update-slice_fusion.4
  226.7 0.0 copy-done.2
  226.8 1.6 dynamic-slice_multiply_fusion
  228.4 2.9 copy.17
  231.2 94.4 %all-gather.3.cloned.1.call-done = bf16[1024,4096]{1,0:T(8,128)(2,1)} async-done(((bf16[128,4096]{1,0:T(8,128)(2,1)}), bf16[1024,4096]{1,0:T(8,128)(2,1)}) %all-gather.3.cloned.1.call-update) | async-done | bytes 8388624 | tf_op jit(solution)/shard_map/all_gather | solution.py:34
  325.6 6.6 %convolution_convert_fusion = bf16[256,1024]{1,0:T(8,128)(2,1)} fusion(bf16[256,4096]{0,1:T(8,128)(2,1)S(1)} %copy-done.1, bf16[1024,4096]{1,0:T(8,128)(2,1)} %all-gather.3.cloned.1.call-done), kind=kOutput, calls=%fused_computation.10 | convolution fusion | flops 2147745792 | bytes 11010048 | tf_op jit(solution)/shard_map/dot_general | solution.py:32
  (15 shorter events, 0.3 us)
Async XLA Ops:
  7.2 97.8 %all-gather.5.cloned.1.call-start = ((), (), s32[]{:S(2)}) async-start(), calls=%async_computation.3 | async-start | bytes 2621440 | tf_op jit(solution)/shard_map/all_gather | solution.py:40
  7.9 191.5 %reduce-scatter.2.cloned.1.call-start = ((), (), s32[]{:S(2)}) async-start(), calls=%async_computation.4 | async-start | bytes 4718592 | tf_op jit(solution)/shard_map/reduce_scatter | solution.py:45
  21.0 4.1 %copy-start.3 = (f32[4096]{0:T(1024)S(1)}, f32[4096]{0:T(1024)}, u32[]{:S(2)}) copy-start(f32[4096]{0:T(1024)} %param.13) | copy-start | bytes 49156
  21.0 4.1 %copy-start.4 = (f32[4096]{0:T(1024)S(1)}, f32[4096]{0:T(1024)}, u32[]{:S(2)}) copy-start(f32[4096]{0:T(1024)} %param.12) | copy-start | bytes 49156
  72.2 1.3 copy-start
  111.5 214.1 %all-gather.3.cloned.1.call-start = ((), (), s32[]{:S(2)}) async-start(), calls=%async_computation.2 | async-start | bytes 9437184 | tf_op jit(solution)/shard_map/all_gather | solution.py:34
  199.4 27.4 %copy-start.2 = (f32[128,1024]{0,1:T(8,128)S(1)}, f32[128,1024]{0,1:T(8,128)}, u32[]{:S(2)}) copy-start(f32[128,1024]{0,1:T(8,128)} %reduce-scatter.2.cloned.1.call-done) | copy-start | bytes 1572868
  199.4 8.8 %collective-permute-start = (f32[128,1024]{0,1:T(8,128)}, f32[128,1024]{0,1:T(8,128)S(1)}, u32[]{:S(2)}, u32[]{:S(2)}) collective-permute-start(f32[128,1024]{0,1:T(8,128)} %reduce-scatter.2.cloned.1.call-done), channel_id=1, source_target_pairs={{0,1},{1,2},{2,3},{3,0},{4,5},{5,6},{6,7},{7,4},{8,9},{9,10},{10,1... | collective-permute-start | bytes 1572872 | tf_op jit(solution)/shard_map/ppermute | solution.py:12
  208.2 8.6 %collective-permute-start.1 = (f32[128,1024]{0,1:T(8,128)S(1)}, f32[128,1024]{0,1:T(8,128)S(1)}, u32[]{:S(2)}, u32[]{:S(2)}) collective-permute-start(f32[128,1024]{0,1:T(8,128)S(1)} %collective-permute-done), channel_id=1, source_target_pairs={{0,1},{1,2},{2,3},{3,0},{4,5},{5,6},{6,7},{7,4},{8,9},{9,10},{10,1... | collective-permute-start | bytes 1572872 | tf_op jit(solution)/shard_map/ppermute | solution.py:12
  216.8 8.6 %collective-permute-start.2 = (f32[128,1024]{0,1:T(8,128)S(1)}, f32[128,1024]{0,1:T(8,128)S(1)}, u32[]{:S(2)}, u32[]{:S(2)}) collective-permute-start(f32[128,1024]{0,1:T(8,128)S(1)} %collective-permute-done.1), channel_id=1, source_target_pairs={{0,1},{1,2},{2,3},{3,0},{4,5},{5,6},{6,7},{7,4},{8,9},{9,10},{10,1... | collective-permute-start | bytes 1572872 | tf_op jit(solution)/shard_map/ppermute | solution.py:12
  226.8 98.8 %copy-start.1 = (bf16[256,4096]{0,1:T(8,128)(2,1)S(1)}, bf16[256,4096]{0,1:T(8,128)(2,1)}, u32[]{:S(2)}) copy-start(bf16[256,4096]{0,1:T(8,128)(2,1)} %copy-done) | copy-start | bytes 6291460
Sparse Core Ops, SparseCore 0:
  9.5 25.2 all-gather.4
  111.6 87.6 reduce-scatter.1
  201.5 124.0 all-gather.2
